TPU v7x, 32 devices: a whole 2x2x4 slice. The times are simulated.
32 devices in a mesh: owner: 16 (over z, x, core), rep: 2 (over y).
Axes of the slice: x: 2, y: 2, z: 4, core: 2. Of those that a mesh axis runs over, the one named last changes fastest.
Arguments:
- features: float32 [16384, 256], P(('owner', 'rep')), may hold values from -6 to 6
- group_ids: int32 [16384], P(('owner', 'rep')), may hold values from 0 to 65535, as said below
- survive: int32 [16384], P(('owner', 'rep')), may hold values from 0 to 1
- home_row: int32 [65536], replicated, may hold values from 0 to 65535, as said below
- hot_ids: int32 [256], replicated, may hold values from 0 to 65535, as said below
Outputs:
- group_out: float32 [65536, 256], P(('owner', 'rep'))
- group_count: float32 [65536], P(('owner', 'rep'))
- hot_out: float32 [256, 256], P('rep')
- hot_count: float32 [256], P('rep')
Inputs may be any that keep to these rules, and one draw needn't show every extreme that they name: home_row is a permutation of the groups. hot_ids holds 256 different groups. `group_ids`: among the rows of one device, 128 name hot groups, and at most 64 rows name non-hot groups g whose home_row[g] // 4096 is one and the same owner index; on every device some owners get exactly 64 such rows.
All inputs are finite; a program needn't handle non-finite values.
Results may differ from a plain program's by a relative error of at most 0.00007.
Values sent between devices are 32-bit elements; how exact they have to be, the bound alone decides.
A program may use at most 64 MiB of HBM per device.

v0:
```python
import functools

import jax
import jax.numpy as jnp
from jax import lax
from jax.experimental import pallas as pl
from jax.experimental.pallas import tpu as pltpu
from jax.sharding import PartitionSpec as P

MESH = pl.DeviceIdType.MESH
LANES = 128
SUB = 8
BF = jnp.bfloat16
F32 = jnp.float32


def iota(shape, axis):
    return lax.broadcasted_iota(jnp.int32, shape, axis)


def mm(a, b, dims=((1,), (0,))):
    return lax.dot_general(a, b, (dims, ((), ())), preferred_element_type=F32)


def split(x):
    hi = x.astype(BF)
    return hi, (x - hi.astype(F32)).astype(BF)


def kernel(
    cfg,
    ids_hbm,
    survive_hbm,
    hot_hbm,
    table_hbm,
    feat_hbm,
    sum_ref,
    count_ref,
    hot_sum_ref,
    hot_count_ref,
    ids_ref,
    survive_ref,
    hot_ref,
    table_ref,
    feat_ref,
    bucket,
    arrived,
    tags,
    tags_in,
    hot_part,
    hot_l1,
    hot_s1,
    hot_l2,
    hot_s2,
    hot_l3,
    hot_red,
    hot_all,
    load,
    send1,
    recv1,
    send2,
    recv2,
    tsend,
    trecv,
    s_core,
    r_core,
    s_rep,
    r_rep,
    s_chip,
    r_chip,
    s_all,
    r_all,
    s_last,
    r_last,
):
    owners, reps, cap, own_groups, home_dev = cfg
    rows, width = feat_ref.shape
    hots = hot_ref.shape[1]
    nb = width // cap
    chunks = owners // nb
    chips = owners // 2
    pieces = hots // reps // 2 // SUB
    part = pieces * SUB
    ndev = owners * reps
    half = owners // 2
    quarter = owners // 4
    me = lax.axis_index("owner")
    rep = lax.axis_index("rep")
    dev = me * reps + rep
    core = lax.rem(me, 2)
    chip = me // 2

    loads = [
        pltpu.make_async_copy(src, dst, load.at[i])
        for i, (src, dst) in enumerate(
            (
                (table_hbm, table_ref),
                (ids_hbm, ids_ref),
                (survive_hbm, survive_ref),
                (hot_hbm, hot_ref),
                (feat_hbm, feat_ref),
            )
        )
    ]
    for copy in loads:
        copy.start()

    barrier = pltpu.get_barrier_semaphore()

    @pl.loop(1, ndev)
    def _(d):
        other = lax.rem(dev + d, ndev)
        pl.semaphore_signal(
            barrier, inc=1, device_id=(other // reps, lax.rem(other, reps)), device_id_type=MESH
        )

    flips = []
    bit = 1
    while bit < owners:
        flips.append((bit, bit - 2 * bit * lax.rem(me // bit, 2)))
        bit *= 2

    def partner(p):
        v = p - half
        number = p if p < half else half + v // 2 + (v % 2) * quarter
        out = me
        for bit, flip in flips:
            if number & bit:
                out = out + flip
        return out

    for copy in loads[:4]:
        copy.wait()
    ids = ids_ref[...]
    live_f = jnp.where(survive_ref[...] == 1, 1.0, 0.0)
    table = table_ref[...]
    trows = table.shape[0]
    halves = jnp.concatenate([table >> 8, table & 255], axis=1).astype(F32).astype(BF)
    pick = jnp.where(iota((trows, rows), 0) == (ids >> 7), 1.0, 0.0).astype(BF)
    both = mm(halves, pick, ((0,), (0,)))
    column = both[:LANES] * 256.0 + both[LANES:]
    home = jnp.sum(
        jnp.where(iota((LANES, rows), 0) == (ids & (LANES - 1)), column, 0.0), axis=0, keepdims=True
    )
    target = jnp.floor(home * (1.0 / own_groups))
    label = home - target * own_groups + 1.0
    number = target.astype(jnp.int32) ^ me
    low = number & (half - 1)
    spread = half + 2 * (low & (quarter - 1)) + jnp.where(low >= quarter, 1, 0)
    place_at = jnp.where(number < half, number, spread)

    hot_col = jnp.sum(
        jnp.where(iota((hots, hots), 0) == iota((hots, hots), 1), hot_ref[...].astype(F32), 0.0),
        axis=1,
        keepdims=True,
    )
    matches = jnp.where(hot_col == ids.astype(F32), 1.0, 0.0)
    is_hot = jnp.max(matches, axis=0, keepdims=True)
    keep = live_f * (1.0 - is_hot)
    place_at = jnp.where(keep > 0.0, place_at, -1)

    member = jnp.where(iota((owners, rows), 0) == place_at, 1.0, 0.0)
    before = jnp.where(iota((rows, rows), 0) < iota((rows, rows), 1), 1.0, 0.0).astype(BF)
    position = mm(member.astype(BF), before)
    placed = jnp.sum(position * member, axis=0, keepdims=True).astype(jnp.int32)
    slot = jnp.where(keep > 0.0, place_at * cap + placed, -1)
    lane = placed + cap * (place_at & (nb - 1))
    label_hi = jnp.floor(label * (1.0 / 256.0))
    label_lo = label - 256.0 * label_hi
    coded = jnp.concatenate([member * label_hi, member * label_lo], axis=0).astype(BF)
    where = jnp.where(iota((width, rows), 0) == lane, 1.0, 0.0).astype(BF)
    coded = mm(coded, where, ((1,), (1,)))
    labels = coded[:owners] * 256.0 + coded[owners:]
    for p in range(owners):
        tags[p] = labels[p : p + 1]

    def send_block(p):
        return pltpu.make_async_remote_copy(
            src_ref=bucket.at[p - 1],
            dst_ref=arrived.at[0, p],
            send_sem=send1,
            recv_sem=recv1.at[p],
            device_id=(partner(p), rep),
            device_id_type=MESH,
        )

    def send_tag(q, p):
        return pltpu.make_async_remote_copy(
            src_ref=tags.at[p],
            dst_ref=tags_in.at[q, p],
            send_sem=tsend.at[q, p],
            recv_sem=trecv.at[q, p],
            device_id=(partner(p), lax.rem(rep + q, reps)),
            device_id_type=MESH,
        )

    def forward(q, p):
        return pltpu.make_async_remote_copy(
            src_ref=arrived.at[0, p],
            dst_ref=arrived.at[q, p],
            send_sem=send2,
            recv_sem=recv2.at[q, p],
            device_id=(me, lax.rem(rep + q, reps)),
            device_id_type=MESH,
        )

    pairs = [(q, p) for p in range(owners) for q in range(reps) if q + p]
    tags_in[0, 0] = labels[:1]
    loads[4].wait()
    feat_hi, feat_lo = split(feat_ref[...])
    mate = (me + 1 - 2 * core, rep)
    to_core = pltpu.make_async_remote_copy(
        src_ref=hot_part.at[:, 1 - core],
        dst_ref=hot_l1,
        send_sem=s_core,
        recv_sem=r_core,
        device_id=mate,
        device_id_type=MESH,
    )
    def hot_start():
        hot_table = matches * live_f
        tally = jnp.sum(hot_table, axis=1, keepdims=True)
        hot_bf = hot_table.astype(BF)
        sums = mm(hot_bf, feat_hi) + mm(hot_bf, feat_lo)
        hot_part[:, :, :, :width] = sums.reshape(reps, 2, part, width)
        hot_part[:, :, :, width:] = jnp.broadcast_to(tally, (hots, LANES)).reshape(reps, 2, part, LANES)
        to_core.start()

    for c in range(chunks):
        place = jnp.where(iota((width, rows), 0) + c * width == slot, 1.0, 0.0).astype(BF)
        packed = mm(place, feat_hi) + mm(place, feat_lo)
        for i in range(nb):
            p = c * nb + i
            dst = arrived.at[0, 0] if p == 0 else bucket.at[p - 1]
            dst[...] = packed[i * cap : (i + 1) * cap]
        if c == 0:
            pl.semaphore_wait(barrier, ndev - 1)
        for p in range(c * nb, (c + 1) * nb):
            if p == 0:
                for q in range(1, reps):
                    forward(q, 0).start()
            elif c < chunks - 1:
                send_block(p).start()
        if c == chunks - 2:
            hot_start()
    for q, p in pairs:
        send_tag(q, p).start()

    def to_rep(q):
        other = lax.rem(rep + q, reps)
        return pltpu.make_async_remote_copy(
            src_ref=hot_s1.at[other],
            dst_ref=hot_l2.at[q],
            send_sem=s_rep.at[q],
            recv_sem=r_rep.at[q],
            device_id=(me, other),
            device_id_type=MESH,
        )

    def to_chip(p):
        return pltpu.make_async_remote_copy(
            src_ref=hot_s2.at[p],
            dst_ref=hot_l3.at[lax.rem(p - chip + chips, chips)],
            send_sem=s_chip.at[p],
            recv_sem=r_chip,
            device_id=(p * 2 + core, rep),
            device_id_type=MESH,
        )

    def to_all(d):
        return pltpu.make_async_remote_copy(
            src_ref=hot_red,
            dst_ref=hot_all.at[core, chip],
            send_sem=s_all.at[d],
            recv_sem=r_all.at[chip],
            device_id=(lax.rem(chip + d, chips) * 2 + core, rep),
            device_id_type=MESH,
        )

    to_mate = pltpu.make_async_remote_copy(
        src_ref=hot_all.at[core],
        dst_ref=hot_all.at[core],
        send_sem=s_last,
        recv_sem=r_last,
        device_id=mate,
        device_id_type=MESH,
    )

    def hot_step_1():
        to_core.wait_recv()
        hot_s1[...] = hot_part[:, core] + hot_l1[...]
        for q in range(1, reps):
            to_rep(q).start()

    def hot_step_2():
        total = hot_s1[rep]
        for q in range(1, reps):
            to_rep(q).wait_recv()
            total = total + hot_l2[q]
        hot_s2[...] = total.reshape(pieces, SUB, width + LANES)

        @pl.loop(0, pieces)
        def _(p):
            @pl.when(p != chip)
            def _():
                to_chip(p).start()

    def hot_step_3():
        @pl.when(chip < pieces)
        def _():
            mine = hot_l3.at[pl.ds(1, chips - 1)]
            pltpu.make_async_copy(mine, mine, r_chip).wait()
            total = hot_s2[chip] + jnp.sum(hot_l3[1:], axis=0)
            hot_red[...] = total
            hot_all[core, chip] = total

            @pl.loop(1, chips)
            def _(d):
                to_all(d).start()

    def hot_step_4():
        @pl.loop(0, pieces)
        def _(p):
            @pl.when(p != chip)
            def _():
                pltpu.make_async_copy(hot_all.at[core, p], hot_all.at[core, p], r_all.at[p]).wait()

        to_mate.start()

    def hot_step_5():
        to_mate.wait_recv()
        everything = hot_all[...].reshape(2 * part, width + LANES)
        hot_sum_ref[...] = everything[:, :width]
        counts = everything[:, width:]
        diagonal = jnp.where(iota((2 * part, LANES), 0) == iota((2 * part, LANES), 1), counts, 0.0)
        hot_count_ref[...] = jnp.broadcast_to(jnp.sum(diagonal, axis=0, keepdims=True), (SUB, LANES))

    tiles = max(1, home_dev // 512)
    tile = home_dev // tiles
    base = rep * home_dev + 1

    def add_chunk(q, c):
        first = q == 0 and c == 0
        lab = jnp.zeros((1, width), F32)
        for p in range(c * nb, (c + 1) * nb):
            if q + p:
                send_tag(q, p).wait_recv()
            lab = lab + tags_in[q, p]
        lab = lab.astype(jnp.int32) - base
        block = jnp.concatenate([arrived[q, c * nb + i] for i in range(nb)], axis=0)
        hi, lo = split(block)
        ones = jnp.ones((SUB, width), BF)

        for t in range(tiles):
            onehot = jnp.where(iota((tile, width), 0) + t * tile == lab, 1.0, 0.0).astype(BF)
            at = pl.ds(t * tile, tile)
            total = mm(onehot, hi) + mm(onehot, lo)
            tally = mm(ones, onehot, ((1,), (1,)))
            if first:
                sum_ref[at, :] = total
                count_ref[:, at] = tally
            else:
                sum_ref[at, :] += total
                count_ref[:, at] += tally

    def pass_on(c):
        for p in range(max(1, c * nb), (c + 1) * nb):
            send_block(p).wait_recv()
            for q in range(1, reps):
                forward(q, p).start()

    def peer_chunk(c):
        for q in range(1, reps):
            for p in range(c * nb, (c + 1) * nb):
                forward(q, p).wait_recv()
            add_chunk(q, c)

    hot_step_1()
    pass_on(0)
    add_chunk(0, 0)
    hot_step_2()
    for p in range((chunks - 1) * nb, owners):
        send_block(p).start()
    for c in range(1, chunks - 1):
        pass_on(c)
        if c < chunks - 2:
            add_chunk(0, c)
    hot_step_3()
    pass_on(chunks - 1)
    for c in range(chunks - 2, chunks):
        add_chunk(0, c)
    hot_step_4()
    for c in range(chunks - 1):
        peer_chunk(c)
    hot_step_5()
    peer_chunk(chunks - 1)

    to_core.wait_send()
    for q in range(1, reps):
        to_rep(q).wait_send()

    @pl.loop(0, pieces)
    def _(p):
        @pl.when(p != chip)
        def _():
            to_chip(p).wait_send()

    @pl.when(chip < pieces)
    def _():
        @pl.loop(1, chips)
        def _(d):
            to_all(d).wait_send()

    to_mate.wait_send()
    for q, p in pairs:
        send_tag(q, p).wait_send()
    pltpu.make_async_copy(bucket, bucket, send1).wait()
    if reps > 1:
        sent = arrived.at[pl.ds(1, reps - 1)]
        pltpu.make_async_copy(sent, sent, send2).wait()


def local(features, group_ids, survive, home_row, hot_ids):
    rows, width = features.shape
    owners = lax.axis_size("owner")
    reps = lax.axis_size("rep")
    groups = home_row.shape[0]
    hots = hot_ids.shape[0]
    own_groups = groups // owners
    home_dev = own_groups // reps
    cap = 2 * rows // owners
    chips = owners // 2
    pieces = hots // reps // 2 // SUB
    part = pieces * SUB
    wide = width + LANES
    cfg = (owners, reps, cap, own_groups, home_dev)
    vmem = pl.BlockSpec(memory_space=pltpu.VMEM)
    hbm = pl.BlockSpec(memory_space=pltpu.HBM)
    DMA = pltpu.SemaphoreType.DMA
    VM = pltpu.VMEM
    cold_sum, count, hot_sum, hot_count = pl.pallas_call(
        functools.partial(kernel, cfg),
        out_shape=(
            jax.ShapeDtypeStruct((home_dev, width), F32),
            jax.ShapeDtypeStruct((SUB, home_dev), F32),
            jax.ShapeDtypeStruct((hots // reps, width), F32),
            jax.ShapeDtypeStruct((SUB, LANES), F32),
        ),
        in_specs=[hbm] * 5,
        out_specs=[vmem] * 4,
        scratch_shapes=[
            VM((1, rows), jnp.int32),
            VM((1, rows), jnp.int32),
            VM((1, hots), jnp.int32),
            VM((groups // LANES, LANES), jnp.int32),
            VM((rows, width), F32),
            VM((owners - 1, cap, width), F32),
            VM((reps, owners, cap, width), F32),
            VM((owners, 1, width), F32),
            VM((reps, owners, 1, width), F32),
            VM((reps, 2, part, wide), F32),
            VM((reps, part, wide), F32),
            VM((reps, part, wide), F32),
            VM((reps, part, wide), F32),
            VM((pieces, SUB, wide), F32),
            VM((chips, SUB, wide), F32),
            VM((SUB, wide), F32),
            VM((2, pieces, SUB, wide), F32),
            DMA((5,)),
            DMA(()),
            DMA((owners,)),
            DMA(()),
            DMA((reps, owners)),
            DMA((reps, owners)),
            DMA((reps, owners)),
            DMA(()),
            DMA(()),
            DMA((reps,)),
            DMA((reps,)),
            DMA((pieces,)),
            DMA(()),
            DMA((chips,)),
            DMA((pieces,)),
            DMA(()),
            DMA(()),
        ],
        compiler_params=pltpu.CompilerParams(
            collective_id=0, has_side_effects=True, vmem_limit_bytes=48 << 20
        ),
    )(
        group_ids.reshape(1, rows),
        survive.reshape(1, rows),
        hot_ids.reshape(1, hots),
        home_row.reshape(groups // LANES, LANES),
        features,
    )
    group_count = count[0]
    counts_hot = hot_count[0, : hots // reps]
    group_out = cold_sum / jnp.sqrt(1.0 + group_count)[:, None]
    hot_out = hot_sum / jnp.sqrt(1.0 + counts_hot)[:, None]
    return group_out, group_count, hot_out, counts_hot


def solution(mesh):
    in_specs = (P(("owner", "rep"), None), P(("owner", "rep")), P(("owner", "rep")), P(), P())
    out_specs = (P(("owner", "rep"), None), P(("owner", "rep")), P("rep", None), P("rep"))
    return jax.shard_map(local, mesh=mesh, in_specs=in_specs, out_specs=out_specs, check_vma=False)
```

profile of v0, /device:TPU:0, one launch (start us, length us, event | category | flops | bytes accessed | tf_op | source)
XLA Modules:
  0.0 49.5 jit_solution(5555162463847758923)
XLA Ops:
  0.6 0.0 copy-start
  0.6 1.0 %copy-done = f32[512,256]{1,0:T(8,128)S(1)} copy-done((f32[512,256]{1,0:T(8,128)S(1)}, f32[512,256]{1,0:T(8,128)}, u32[]{:S(2)}) %copy-start) | copy-done | bytes 524312
  1.7 0.0 copy-start.1
  1.7 0.9 %copy-done.1 = s32[65536]{0:T(1024)S(1)} copy-done((s32[65536]{0:T(1024)S(1)}, s32[65536]{0:T(1024)}, u32[]{:S(2)}) %copy-start.1) | copy-done | bytes 262168
  2.6 0.0 copy-start.2
  2.6 0.7 %copy-done.2 = s32[512]{0:T(512)S(1)} copy-done((s32[512]{0:T(512)S(1)}, s32[512]{0:T(512)}, u32[]{:S(2)}) %copy-start.2) | copy-done | bytes 2072
  3.3 0.0 copy-start.3
  3.3 0.7 %copy-done.3 = s32[512]{0:T(512)S(1)} copy-done((s32[512]{0:T(512)S(1)}, s32[512]{0:T(512)}, u32[]{:S(2)}) %copy-start.3) | copy-done | bytes 2072
  4.0 0.0 copy-start.4
  4.0 0.7 %copy-done.4 = s32[256]{0:T(256)S(1)} copy-done((s32[256]{0:T(256)S(1)}, s32[256]{0:T(256)}, u32[]{:S(2)}) %copy-start.4) | copy-done | bytes 1048
  4.7 41.9 %shard_map.84 = (f32[2048,256]{1,0:T(8,128)S(1)}, f32[8,2048]{1,0:T(8,128)S(1)}, f32[128,256]{1,0:T(8,128)S(1)}, f32[8,128]{1,0:T(8,128)S(1)}) custom-call(s32[1,512]{1,0:T(1,128)S(1)} %bitcast.9, s32[1,512]{1,0:T(1,128)S(1)} %bitcast.10, s32[1,256]{1,0:T(1,128)S(1)} %bitcast.11, s32[512,128]{1,0:T(8,128)S(1)} %bitcast.8, f32[512,256]{1,0:T(8,128)S(1)} %copy-done), custom_call_target="tpu_custom_call" | custom-call | tf_op jit(solution)/shard_map/pallas_call | solution.py:441
  46.5 0.5 %add_sqrt_fusion.1 = (f32[128]{0:T(128)S(1)}, f32[128]{0:T(128)}) fusion(f32[8,128]{1,0:T(8,128)S(1)} %get-tuple-element.11), kind=kLoop, calls=%fused_computation.3 | loop fusion | flops 128 | bytes 1536 | tf_op jit(solution)/shard_map/sqrt | solution.py:500
  47.1 0.7 %broadcast_divide_fusion.1 = f32[128,256]{1,0:T(8,128)} fusion(f32[128,256]{1,0:T(8,128)S(1)} %get-tuple-element.10, f32[128]{0:T(128)S(1)} %get-tuple-element.12), kind=kLoop, calls=%fused_computation.1 | loop fusion | flops 32768 | bytes 262656 | tf_op jit(solution)/shard_map/div | solution.py:500
  47.8 0.0 copy-start.5
  47.8 1.7 %broadcast_divide_fusion = f32[2048,256]{1,0:T(8,128)} fusion(f32[2048,256]{1,0:T(8,128)S(1)} %get-tuple-element.8, f32[2048]{0:T(1024)S(1)} %add_sqrt_fusion), kind=kLoop, calls=%fused_computation | loop fusion | flops 524288 | bytes 4202496 | tf_op jit(solution)/shard_map/div | solution.py:499
  49.5 0.0 copy-done.5
  (2 shorter events, 0.0 us)
Async XLA Ops:
  0.6 1.0 %copy-start = (f32[512,256]{1,0:T(8,128)S(1)}, f32[512,256]{1,0:T(8,128)}, u32[]{:S(2)}) copy-start(f32[512,256]{1,0:T(8,128)} %feat_hbm.1) | copy-start | bytes 1572868
  1.7 0.9 %copy-start.1 = (s32[65536]{0:T(1024)S(1)}, s32[65536]{0:T(1024)}, u32[]{:S(2)}) copy-start(s32[65536]{0:T(1024)} %param.8) | copy-start | bytes 786436
  2.6 0.7 %copy-start.2 = (s32[512]{0:T(512)S(1)}, s32[512]{0:T(512)}, u32[]{:S(2)}) copy-start(s32[512]{0:T(512)} %param.6) | copy-start | bytes 6148
  3.3 0.7 %copy-start.3 = (s32[512]{0:T(512)S(1)}, s32[512]{0:T(512)}, u32[]{:S(2)}) copy-start(s32[512]{0:T(512)} %param.7) | copy-start | bytes 6148
  4.0 0.7 %copy-start.4 = (s32[256]{0:T(256)S(1)}, s32[256]{0:T(256)}, u32[]{:S(2)}) copy-start(s32[256]{0:T(256)} %param.9) | copy-start | bytes 3076
  47.8 1.7 %copy-start.5 = (f32[1,2048]{1,0:T(1,128)}, f32[1,2048]{1,0:T(1,128)S(1)}, u32[]{:S(2)}) copy-start(f32[1,2048]{1,0:T(1,128)S(1)} %slice.6) | copy-start | bytes 24580
where the time goes:
time: 49.8 us; the launch traced here: 49.5 us
  Pallas kernels  41.9 us (84%)
  local copies, waits for them, and re-layouts  4.03 us (8%)
  other arithmetic  2.93 us (6%)
  between operations  0.66 us (1%)
    pallas_call x1, Pallas kernels, local(): pl.pallas_call(functools.partial(kernel, cfg), out_shape=(jax.ShapeDtypeS...  41.9 us
    unnamed x12, local copies, waits for them, and re-layouts  4.03 us
    div x1, other arithmetic, local(): group_out = cold_sum / jnp.sqrt(1.0 + group_count)[:, None]  1.67 us

commit v1 on v0

v1 whole, which is shorter than its diff:
```python
import functools

import jax
import jax.numpy as jnp
from jax import lax
from jax.experimental import pallas as pl
from jax.experimental.pallas import tpu as pltpu
from jax.sharding import PartitionSpec as P

MESH = pl.DeviceIdType.MESH
LANES = 128
SUB = 8
BF = jnp.bfloat16
F32 = jnp.float32


def iota(shape, axis):
    return lax.broadcasted_iota(jnp.int32, shape, axis)


def mm(a, b, dims=((1,), (0,))):
    return lax.dot_general(a, b, (dims, ((), ())), preferred_element_type=F32)


def split(x):
    hi = x.astype(BF)
    return hi, (x - hi.astype(F32)).astype(BF)


def onehot(mask):
    return jnp.where(mask, 1.0, 0.0).astype(BF)


def log2(n):
    return n.bit_length() - 1


class Sizes:
    def __init__(self, owners, reps, rows, width, groups, hots):
        self.owners, self.reps, self.rows, self.width, self.hots = owners, reps, rows, width, hots
        self.groups = groups
        self.own_groups = groups // owners
        self.home_dev = self.own_groups // reps
        self.cap = 2 * rows // owners
        self.nb = width // self.cap
        self.pair = LANES // self.cap
        self.pairs = owners // self.pair
        self.chips = owners // 2
        self.part = hots // reps // 2
        self.near = min(self.chips // 2, self.part // SUB)
        self.far = self.chips // self.near
        self.piece = self.part // self.near
        self.home_rows = self.home_dev // LANES


def kernel(
    s,
    ids_hbm,
    survive_hbm,
    hot_hbm,
    table_hbm,
    feat_hbm,
    sum_ref,
    count_ref,
    hot_sum_ref,
    hot_count_ref,
    ids_ref,
    survive_ref,
    hot_ref,
    table_ref,
    feat_ref,
    bucket,
    arrived,
    tags,
    tags_in,
    scale_ref,
    hot_part,
    hot_l1,
    hot_s1,
    hot_l2,
    hot_s2,
    hot_l3,
    hot_s3,
    hot_l4,
    hot_s4,
    hot_all,
    half_ref,
    halves_ref,
    load,
    send1,
    recv1,
    send2,
    recv2,
    tsend,
    trecv,
    tsend2,
    trecv2,
    hsend,
    h_core,
    h_near,
    h_rep,
    h_far,
    h_all,
    h_last,
    h_half,
):
    owners, reps, cap, nb = s.owners, s.reps, s.cap, s.nb
    rows, width, hots = s.rows, s.width, s.hots
    me = lax.axis_index("owner")
    rep = lax.axis_index("rep")
    core = lax.rem(me, 2)
    near = lax.rem(me // 2, s.near)

    loads = [
        pltpu.make_async_copy(src, dst, load.at[i])
        for i, (src, dst) in enumerate(
            (
                (table_hbm, table_ref),
                (ids_hbm, ids_ref),
                (survive_hbm, survive_ref),
                (hot_hbm, hot_ref),
                (feat_hbm, feat_ref),
            )
        )
    ]
    for copy in loads:
        copy.start()

    barrier = pltpu.get_barrier_semaphore()

    @pl.loop(1, owners)
    def _(d):
        pl.semaphore_signal(
            barrier, inc=1, device_id=(lax.rem(me + d, owners), rep), device_id_type=MESH
        )

    @pl.loop(1, reps)
    def _(d):
        pl.semaphore_signal(
            barrier, inc=1, device_id=(me, lax.rem(rep + d, reps)), device_id_type=MESH
        )

    flips = []
    bit = 1
    while bit < owners:
        flips.append((bit, bit - 2 * bit * lax.rem(me // bit, 2)))
        bit *= 2

    def partner(p):
        out = me
        for bit, flip in flips:
            if p & bit:
                out = out + flip
        return out

    def other_rep(q):
        return lax.rem(rep + q, reps)

    def remote(src, dst, send, recv, device):
        return pltpu.make_async_remote_copy(
            src_ref=src,
            dst_ref=dst,
            send_sem=send,
            recv_sem=recv,
            device_id=device,
            device_id_type=MESH,
        )

    for copy in loads[:4]:
        copy.wait()
    ids = ids_ref[...]
    live_f = jnp.where(survive_ref[...] == 1, 1.0, 0.0)
    table = table_ref[...]
    trows = table.shape[0]
    halves = jnp.concatenate([table >> 8, table & 255], axis=1).astype(F32).astype(BF)
    pick = onehot(iota((trows, rows), 0) == (ids >> 7))
    both = mm(halves, pick, ((0,), (0,)))
    column = both[:LANES] * 256.0 + both[LANES:]
    home = jnp.sum(
        jnp.where(iota((LANES, rows), 0) == (ids & (LANES - 1)), column, 0.0), axis=0, keepdims=True
    )
    target = jnp.floor(home * (1.0 / s.own_groups))
    label = home - target * s.own_groups + 1.0
    place_at = target.astype(jnp.int32) ^ me

    at = iota((hots, hots), 0)
    block = at >> log2(s.piece)
    number = (
        (block & (reps - 1)) * (2 * s.part)
        + (block >> log2(reps)) * s.piece
        + (at & (s.piece - 1))
    )
    hot_col = jnp.sum(
        jnp.where(number == iota((hots, hots), 1), hot_ref[...].astype(F32), 0.0),
        axis=1,
        keepdims=True,
    )
    matches = jnp.where(hot_col == ids.astype(F32), 1.0, 0.0)
    is_hot = jnp.max(matches, axis=0, keepdims=True)
    keep = live_f * (1.0 - is_hot)
    place_at = jnp.where(keep > 0.0, place_at, -1)

    member = jnp.where(iota((owners, rows), 0) == place_at, 1.0, 0.0)
    before = onehot(iota((rows, rows), 0) < iota((rows, rows), 1))
    position = mm(member.astype(BF), before)
    placed = jnp.sum(position * member, axis=0, keepdims=True).astype(jnp.int32)
    slot = jnp.where(keep > 0.0, place_at * cap + placed, -1)

    def make_tags():
        lane = placed + cap * (place_at & (s.pair - 1))
        label_hi = jnp.floor(label * (1.0 / 256.0))
        label_lo = label - 256.0 * label_hi
        coded = jnp.concatenate([member * label_hi, member * label_lo], axis=0).astype(BF)
        where = onehot(iota((LANES, rows), 0) == lane)
        coded = mm(coded, where, ((1,), (1,)))
        labels = coded[:owners] * 256.0 + coded[owners:]
        lives = jnp.broadcast_to(live_f, (SUB, rows)).astype(BF)
        counts = mm(lives, matches.astype(BF), ((1,), (1,)))[:1]
        half = hots // 2
        same = jnp.where(core == 0, counts[:, :half], counts[:, half:])
        flipped = jnp.where(core == 0, counts[:, half:], counts[:, :half])
        for p in range(owners):
            tags[p, :, :LANES] = labels[p : p + 1]
            tags[p, :, LANES:] = same if p % 2 == 0 else flipped
        tags_in[0, 0] = tags[0]

    def send_block(p):
        return remote(bucket.at[p - 1], arrived.at[0, p], send1, recv1.at[p], (partner(p), rep))

    def forward(q, p):
        return remote(
            arrived.at[0, p], arrived.at[q, p], send2, recv2.at[q, p], (me, other_rep(q))
        )

    def send_tag(p):
        return remote(tags.at[p], tags_in.at[0, p], tsend, trecv.at[p], (partner(p), rep))

    def pass_tags(q):
        return remote(tags_in.at[0], tags_in.at[q], tsend2, trecv2.at[q], (me, other_rep(q)))

    mate = (partner(1), rep)
    to_core = remote(hot_part.at[1 - core], hot_l1, hsend.at[0], h_core, mate)

    def to_near(d):
        there = partner(2 * d)
        index = lax.rem(there // 2, s.near)
        return remote(hot_s1.at[index], hot_l2.at[d], hsend.at[1], h_near.at[d], (there, rep))

    def to_rep(q):
        return remote(
            hot_s2.at[other_rep(q)], hot_l3.at[q], hsend.at[2], h_rep.at[q], (me, other_rep(q))
        )

    def to_far(f):
        return remote(
            hot_s3, hot_l4.at[f], hsend.at[3], h_far.at[f], (partner(2 * s.near * f), rep)
        )

    def to_all(d):
        return remote(
            hot_s4, hot_all.at[core, near], hsend.at[4], h_all.at[near], (partner(2 * d), rep)
        )

    def from_all(d):
        index = lax.rem(partner(2 * d) // 2, s.near)
        piece = hot_all.at[core, index]
        return pltpu.make_async_copy(piece, piece, h_all.at[index])

    to_mate = remote(hot_all.at[core], hot_all.at[core], hsend.at[5], h_last, mate)
    to_half = remote(half_ref, halves_ref.at[core], hsend.at[6], h_half, mate)

    def hot_start():
        hot_bf = (matches * live_f).astype(BF)
        sums = mm(hot_bf, feat_hi) + mm(hot_bf, feat_lo)
        hot_part[...] = sums.reshape(hot_part.shape)
        to_core.start()

    def hot_1():
        to_core.wait_recv()
        hot_s1[...] = hot_part[core] + hot_l1[...]
        for d in range(1, s.near):
            to_near(d).start()

    def hot_2():
        total = hot_s1[near]
        for d in range(1, s.near):
            to_near(d).wait_recv()
            total = total + hot_l2[d]
        hot_s2[...] = total
        for q in range(1, reps):
            to_rep(q).start()

    def hot_3():
        total = hot_s2[rep]
        for q in range(1, reps):
            to_rep(q).wait_recv()
            total = total + hot_l3[q]
        hot_s3[...] = total
        for f in range(1, s.far):
            to_far(f).start()

    def hot_4():
        total = hot_s3[...]
        for f in range(1, s.far):
            to_far(f).wait_recv()
            total = total + hot_l4[f]
        hot_s4[...] = total
        hot_all[core, near] = total
        for d in range(1, s.near):
            to_all(d).start()

    def hot_5():
        for d in range(1, s.near):
            from_all(d).wait()
        to_mate.start()

    def hot_6():
        to_half.wait_recv()
        mine = hots // reps
        j = iota((mine, LANES), 0)
        lane = (
            ((j & (s.part - 1)) >> log2(s.piece)) * (reps * s.piece)
            + rep * s.piece
            + (j & (s.piece - 1))
        )
        source = jnp.where(j < s.part, halves_ref[0], halves_ref[1])
        column = jnp.sum(
            jnp.where(iota((mine, LANES), 1) == lane, source, 0.0), axis=1, keepdims=True
        )
        hot_count_ref[...] = jnp.sum(
            jnp.where(iota((mine, mine), 0) == iota((mine, mine), 1), column, 0.0),
            axis=0,
            keepdims=True,
        )
        to_mate.wait_recv()
        everything = hot_all[...].reshape(mine, width)
        hot_sum_ref[...] = everything * (1.0 / jnp.sqrt(1.0 + column))

    base = rep * s.home_dev + 1

    def labels_of(q, g):
        lab = tags_in[q, g * s.pair, :, :LANES]
        for p in range(g * s.pair + 1, (g + 1) * s.pair):
            lab = lab + tags_in[q, p, :, :LANES]
        return lab.astype(jnp.int32) - base

    tiles = max(1, s.home_dev // 512)
    tile = s.home_dev // tiles

    def add(q, g, first=False, last=False):
        lab = labels_of(q, g)
        blocks = [arrived[q, g * s.pair + i] for i in range(s.pair)]
        hi, lo = split(jnp.concatenate(blocks, axis=0))
        both = jnp.concatenate([hi, lo], axis=0)
        for t in range(tiles):
            here = onehot(iota((tile, LANES), 0) + t * tile == lab)
            at = pl.ds(t * tile, tile)
            total = mm(jnp.concatenate([here, here], axis=1), both)
            if not first:
                total = sum_ref[at, :] + total
            if last:
                scale = scale_ref[at, :]
                total = total * jnp.concatenate([scale] * (width // LANES), axis=1)
            sum_ref[at, :] = total

    def pass_on(p):
        if p:
            send_block(p).wait_recv()
        for q in range(1, reps):
            forward(q, p).start()

    def tags_done():
        for p in range(1, owners):
            send_tag(p).wait_recv()
        for q in range(1, reps):
            pass_tags(q).start()

    def counts_done():
        for q in range(1, reps):
            pass_tags(q).wait_recv()
        total = jnp.sum(tags_in[...].reshape(reps * owners, width), axis=0, keepdims=True)
        half_ref[...] = total[:, LANES:]
        halves_ref[core] = total[:, LANES:]
        to_half.start()
        lab = jnp.concatenate(
            [labels_of(q, g) for q in range(reps) for g in range(s.pairs)], axis=1
        )
        n = lab.shape[1]
        up = max(SUB, s.home_rows)
        high = onehot(iota((up, n), 0) == (lab >> 7))
        low = onehot(iota((LANES, n), 0) == (lab & (LANES - 1)))
        count = mm(high, low, ((1,), (1,)))
        count_ref[...] = count[: s.home_rows]
        scale = 1.0 / jnp.sqrt(1.0 + count)
        for k in range(s.home_rows):
            wide = jnp.broadcast_to(scale[k : k + 1], (LANES, LANES))
            scale_ref[k * LANES : (k + 1) * LANES] = wide.T

    def peers(g, last=False):
        for q in range(1, reps):
            for p in range(g * s.pair, (g + 1) * s.pair):
                forward(q, p).wait_recv()
            add(q, g, last=last and q == reps - 1)

    chunks = owners // nb
    half = owners // 2
    held = range(owners - owners // 8, owners)
    make_tags()
    loads[4].wait()
    feat_hi, feat_lo = split(feat_ref[...])
    for c in range(chunks):
        place = onehot(iota((width, rows), 0) + c * width == slot)
        packed = mm(place, feat_hi) + mm(place, feat_lo)
        for i in range(nb):
            p = c * nb + i
            dst = arrived.at[0, 0] if p == 0 else bucket.at[p - 1]
            dst[...] = packed[i * cap : (i + 1) * cap]
        if c == 0:
            pl.semaphore_wait(barrier, owners + reps - 2)
        for p in range(c * nb, (c + 1) * nb):
            if p == 0:
                pass_on(0)
            elif p not in held:
                send_block(p).start()
        if c == 0:
            for p in range(1, owners):
                send_tag(p).start()
        if c == 1:
            hot_start()

    quarter = half // 2
    pairs = s.pairs
    for p in range(1, quarter):
        pass_on(p)
    hot_1()
    for p in range(quarter, half):
        pass_on(p)
    tags_done()
    for g in range(pairs // 4):
        add(0, g, first=g == 0)
    hot_2()
    for g in range(pairs // 4, pairs // 2):
        add(0, g)
    hot_3()
    for p in held:
        send_block(p).start()
    counts_done()
    peers(0)
    for g in range(pairs // 2, pairs):
        for p in range(g * s.pair, (g + 1) * s.pair):
            pass_on(p)
        if g == pairs // 2:
            hot_4()
        if g == pairs - 2:
            hot_5()
        if g > pairs // 2:
            add(0, g - 1)
            peers(g - pairs // 2)
    add(0, pairs - 1)
    hot_6()
    for g in range(pairs // 2, pairs):
        peers(g, last=g == pairs - 1)

    to_core.wait_send()
    for d in range(1, s.near):
        to_near(d).wait_send()
        to_all(d).wait_send()
    for q in range(1, reps):
        to_rep(q).wait_send()
        pass_tags(q).wait_send()
    for f in range(1, s.far):
        to_far(f).wait_send()
    to_mate.wait_send()
    to_half.wait_send()
    sent = tags.at[pl.ds(1, owners - 1)]
    pltpu.make_async_copy(sent, sent, tsend).wait()
    pltpu.make_async_copy(bucket, bucket, send1).wait()
    if reps > 1:
        sent = arrived.at[pl.ds(1, reps - 1)]
        pltpu.make_async_copy(sent, sent, send2).wait()


def local(features, group_ids, survive, home_row, hot_ids):
    rows, width = features.shape
    groups, hots = home_row.shape[0], hot_ids.shape[0]
    s = Sizes(lax.axis_size("owner"), lax.axis_size("rep"), rows, width, groups, hots)
    owners, reps = s.owners, s.reps
    vmem = pl.BlockSpec(memory_space=pltpu.VMEM)
    hbm = pl.BlockSpec(memory_space=pltpu.HBM)
    DMA = pltpu.SemaphoreType.DMA
    VM = pltpu.VMEM
    operands = (
        group_ids.reshape(1, rows),
        survive.reshape(1, rows),
        hot_ids.reshape(1, hots),
        home_row.reshape(groups // LANES, LANES),
        features,
    )
    operands = [pltpu.with_memory_space_constraint(x, pltpu.HBM) for x in operands]
    cold_sum, count, hot_sum, hot_count = pl.pallas_call(
        functools.partial(kernel, s),
        out_shape=(
            pltpu.VMEM((s.home_dev, width), F32),
            pltpu.VMEM((s.home_rows, LANES), F32),
            pltpu.VMEM((hots // reps, width), F32),
            pltpu.VMEM((1, hots // reps), F32),
        ),
        in_specs=[hbm] * 5,
        out_specs=[vmem] * 4,
        scratch_shapes=[
            VM((1, rows), jnp.int32),
            VM((1, rows), jnp.int32),
            VM((1, hots), jnp.int32),
            VM((groups // LANES, LANES), jnp.int32),
            VM((rows, width), F32),
            VM((owners - 1, s.cap, width), F32),
            VM((reps, owners, s.cap, width), F32),
            VM((owners, 1, width), F32),
            VM((reps, owners, 1, width), F32),
            VM((s.home_dev, LANES), F32),
            VM((2, s.near, reps, s.piece, width), F32),
            VM((s.near, reps, s.piece, width), F32),
            VM((s.near, reps, s.piece, width), F32),
            VM((s.near, reps, s.piece, width), F32),
            VM((reps, s.piece, width), F32),
            VM((reps, s.piece, width), F32),
            VM((s.piece, width), F32),
            VM((s.far, s.piece, width), F32),
            VM((s.piece, width), F32),
            VM((2, s.near, s.piece, width), F32),
            VM((1, LANES), F32),
            VM((2, 1, LANES), F32),
            DMA((5,)),
            DMA(()),
            DMA((owners,)),
            DMA(()),
            DMA((reps, owners)),
            DMA(()),
            DMA((owners,)),
            DMA(()),
            DMA((reps,)),
            DMA((7,)),
            DMA(()),
            DMA((s.near,)),
            DMA((reps,)),
            DMA((s.far,)),
            DMA((s.near,)),
            DMA(()),
            DMA(()),
        ],
        compiler_params=pltpu.CompilerParams(
            collective_id=0, has_side_effects=True, vmem_limit_bytes=48 << 20
        ),
    )(*operands)
    return cold_sum, count.reshape(s.home_dev), hot_sum, hot_count.reshape(hots // reps)


def solution(mesh):
    in_specs = (P(("owner", "rep"), None), P(("owner", "rep")), P(("owner", "rep")), P(), P())
    out_specs = (P(("owner", "rep"), None), P(("owner", "rep")), P("rep", None), P("rep"))
    return jax.shard_map(local, mesh=mesh, in_specs=in_specs, out_specs=out_specs, check_vma=False)
```

time: 49.8 us -> 45.8 us (0.920)
  other arithmetic: 2.93 us -> 0 us
  local copies, waits for them, and re-layouts: 4.03 us -> 3.09 us
    div x2 -> x0, other arithmetic: 2.41 us -> none  [the longest x1 1.67 us: local(): group_out = cold_sum / jnp.sqrt(1.0 + group_count)[:, None]]
    unnamed x12 -> x4, local copies, waits for them, and re-layouts: 4.03 us -> 3.09 us
    sqrt x2 -> x0, other arithmetic: 0.52 us -> none  [the longest x1 0.51 us: local(): hot_out = hot_sum / jnp.sqrt(1.0 + counts_hot)[:, None]]
where the time goes in v1:
time: 45.8 us; the launch traced here: 45.6 us
  Pallas kernels  41.9 us (91%)
  local copies, waits for them, and re-layouts  3.09 us (7%)
  between operations  0.64 us (1%)
    pallas_call x1, Pallas kernels, local(): pl.pallas_call(functools.partial(kernel, s), out_shape=(pltpu.VMEM((s.hom...  41.9 us
    unnamed x4, local copies, waits for them, and re-layouts  3.09 us

profile of v1, /device:TPU:0, one launch (start us, length us, event | category | flops | bytes accessed | tf_op | source)
XLA Modules:
  0.0 45.6 jit_solution(11332011282632772675)
XLA Ops:
  0.6 41.9 %shard_map.84 = (f32[2048,256]{1,0:T(8,128)S(1)}, f32[16,128]{1,0:T(8,128)S(1)}, f32[128,256]{1,0:T(8,128)S(1)}, f32[1,128]{1,0:T(1,128)S(1)}) custom-call(s32[1,512]{1,0:T(1,128)} %bitcast.9, s32[1,512]{1,0:T(1,128)} %bitcast.10, s32[1,256]{1,0:T(1,128)} %bitcast.11, s32[512,128]{1,0:T(8,128)} %bitcast.8, f32[512,256]{1,0:T(8,128)} %feat_hbm.1), custom_call_target="tpu_custom_call" | custom-call | tf_op jit(solution)/shard_map/pallas_call | solution.py:500
  42.5 1.3 %copy.13 = f32[2048,256]{1,0:T(8,128)} copy(f32[2048,256]{1,0:T(8,128)S(1)} %get-tuple-element.12) | data formatting | bytes 4194304
  43.8 0.6 %copy.14 = f32[2048]{0:T(1024)} copy(f32[2048]{0:T(1024)S(1)} %bitcast.6) | data formatting | bytes 16384
  44.4 0.5 %copy.16 = f32[128]{0:T(128)} copy(f32[128]{0:T(128)S(1)} %bitcast.7) | data formatting | bytes 1024
  45.0 0.7 %copy.15 = f32[128,256]{1,0:T(8,128)} copy(f32[128,256]{1,0:T(8,128)S(1)} %get-tuple-element.14) | data formatting | bytes 262144

commit v2 on v1

--- a/solution.py
+++ b/solution.py
@@ -33,6 +33,16 @@
 
 def log2(n):
     return n.bit_length() - 1
+
+
+PLAN = (
+    "M0", "K0", "B0", "s1", "s2", "s3", "f0", "t0", "K1", "s4", "H0", "s5",
+    "s6", "s7", "K2", "s8", "s9", "K3", "s10", "s11", "f1", "f2", "f3", "H1",
+    "s12", "s13", "f4", "f5", "f6", "f7", "T0", "a0", "a1", "a2", "H2", "f11",
+    "a3", "f9", "H3", "s14", "s15", "f10", "f8", "a4", "f12", "f13", "p2", "H4",
+    "p0", "f14", "f15", "a7", "a6", "p1", "p3", "a5", "H5", "p4", "p5", "p6",
+    "C0", "H6", "p7",
+)
 
 
 class Sizes:
@@ -51,6 +61,10 @@
         self.far = self.chips // self.near
         self.piece = self.part // self.near
         self.home_rows = self.home_dev // LANES
+        self.parts = width // LANES
+        self.block = self.parts * self.cap + 1
+        self.hot_block = self.parts * self.piece + 1
+        self.count_rows = max(SUB, self.home_rows)
 
 
 def kernel(
@@ -73,6 +87,7 @@
     arrived,
     tags,
     tags_in,
+    tally_ref,
     scale_ref,
     hot_part,
     hot_l1,
@@ -84,8 +99,6 @@
     hot_l4,
     hot_s4,
     hot_all,
-    half_ref,
-    halves_ref,
     load,
     send1,
     recv1,
@@ -102,7 +115,6 @@
     h_far,
     h_all,
     h_last,
-    h_half,
 ):
     owners, reps, cap, nb = s.owners, s.reps, s.cap, s.nb
     rows, width, hots = s.rows, s.width, s.hots
@@ -206,6 +218,8 @@
     placed = jnp.sum(position * member, axis=0, keepdims=True).astype(jnp.int32)
     slot = jnp.where(keep > 0.0, place_at * cap + placed, -1)
 
+    last_pair = owners - s.pair
+
     def make_tags():
         lane = placed + cap * (place_at & (s.pair - 1))
         label_hi = jnp.floor(label * (1.0 / 256.0))
@@ -214,15 +228,16 @@
         where = onehot(iota((LANES, rows), 0) == lane)
         coded = mm(coded, where, ((1,), (1,)))
         labels = coded[:owners] * 256.0 + coded[owners:]
-        lives = jnp.broadcast_to(live_f, (SUB, rows)).astype(BF)
-        counts = mm(lives, matches.astype(BF), ((1,), (1,)))[:1]
-        half = hots // 2
-        same = jnp.where(core == 0, counts[:, :half], counts[:, half:])
-        flipped = jnp.where(core == 0, counts[:, half:], counts[:, :half])
         for p in range(owners):
-            tags[p, :, :LANES] = labels[p : p + 1]
-            tags[p, :, LANES:] = same if p % 2 == 0 else flipped
-        tags_in[0, 0] = tags[0]
+            block_of(p)[s.block - 1 :] = labels[p : p + 1]
+        for p in range(last_pair, owners):
+            tags[p - last_pair] = labels[p : p + 1]
+
+    def block_of(p):
+        return arrived.at[0, 0] if p == 0 else bucket.at[p - 1]
+
+    def unfold(ref, n):
+        return jnp.concatenate([ref[k * n : (k + 1) * n] for k in range(s.parts)], axis=1)
 
     def send_block(p):
         return remote(bucket.at[p - 1], arrived.at[0, p], send1, recv1.at[p], (partner(p), rep))
@@ -233,7 +248,8 @@
         )
 
     def send_tag(p):
-        return remote(tags.at[p], tags_in.at[0, p], tsend, trecv.at[p], (partner(p), rep))
+        i = p - last_pair
+        return remote(tags.at[i], tags_in.at[0, i], tsend, trecv.at[i], (partner(p), rep))
 
     def pass_tags(q):
         return remote(tags_in.at[0], tags_in.at[q], tsend2, trecv2.at[q], (me, other_rep(q)))
@@ -267,12 +283,21 @@
         return pltpu.make_async_copy(piece, piece, h_all.at[index])
 
     to_mate = remote(hot_all.at[core], hot_all.at[core], hsend.at[5], h_last, mate)
-    to_half = remote(half_ref, halves_ref.at[core], hsend.at[6], h_half, mate)
 
     def hot_start():
         hot_bf = (matches * live_f).astype(BF)
-        sums = mm(hot_bf, feat_hi) + mm(hot_bf, feat_lo)
-        hot_part[...] = sums.reshape(hot_part.shape)
+        sums = mm(hot_bf, feats[0]) + mm(hot_bf, feats[1])
+        lives = jnp.broadcast_to(live_f, (SUB, rows)).astype(BF)
+        counts = mm(lives, hot_bf, ((1,), (1,)))[:1]
+        shape = (2, s.near, reps, s.piece, LANES)
+        for k in range(s.parts):
+            part = sums[:, k * LANES : (k + 1) * LANES].reshape(shape)
+            hot_part[:, :, :, k * s.piece : (k + 1) * s.piece] = part
+        half = hots // 2
+        for c in range(2):
+            for n in range(s.near):
+                for r in range(reps):
+                    hot_part[c, n, r, s.hot_block - 1 :] = counts[:, c * half : (c + 1) * half]
         to_core.start()
 
     def hot_1():
@@ -315,15 +340,22 @@
         to_mate.start()
 
     def hot_6():
-        to_half.wait_recv()
+        to_mate.wait_recv()
         mine = hots // reps
+        order = [(c, n) for c in range(2) for n in range(s.near)]
+        source = jnp.concatenate(
+            [
+                jnp.broadcast_to(hot_all[c, n, s.hot_block - 1 :], (s.piece, LANES))
+                for c, n in order
+            ],
+            axis=0,
+        )
         j = iota((mine, LANES), 0)
         lane = (
             ((j & (s.part - 1)) >> log2(s.piece)) * (reps * s.piece)
             + rep * s.piece
             + (j & (s.piece - 1))
         )
-        source = jnp.where(j < s.part, halves_ref[0], halves_ref[1])
         column = jnp.sum(
             jnp.where(iota((mine, LANES), 1) == lane, source, 0.0), axis=1, keepdims=True
         )
@@ -332,24 +364,32 @@
             axis=0,
             keepdims=True,
         )
-        to_mate.wait_recv()
-        everything = hot_all[...].reshape(mine, width)
+        everything = jnp.concatenate(
+            [unfold(hot_all.at[c, n], s.piece) for c, n in order], axis=0
+        )
         hot_sum_ref[...] = everything * (1.0 / jnp.sqrt(1.0 + column))
 
     base = rep * s.home_dev + 1
 
-    def labels_of(q, g):
-        lab = tags_in[q, g * s.pair, :, :LANES]
-        for p in range(g * s.pair + 1, (g + 1) * s.pair):
-            lab = lab + tags_in[q, p, :, :LANES]
-        return lab.astype(jnp.int32) - base
+    def place_of(rows_of):
+        return functools.reduce(jnp.add, rows_of).astype(jnp.int32) - base
+
+    def tally(lab):
+        high = onehot(iota((s.count_rows, LANES), 0) == (lab >> 7))
+        low = onehot(iota((LANES, LANES), 0) == (lab & (LANES - 1)))
+        return mm(high, low, ((1,), (1,)))
 
     tiles = max(1, s.home_dev // 512)
     tile = s.home_dev // tiles
 
     def add(q, g, first=False, last=False):
-        lab = labels_of(q, g)
-        blocks = [arrived[q, g * s.pair + i] for i in range(s.pair)]
+        own = range(g * s.pair, (g + 1) * s.pair)
+        lab = place_of([arrived[q, p, s.block - 1 :] for p in own])
+        if first:
+            tally_ref[...] = tally(lab)
+        elif g < s.pairs - 1:
+            tally_ref[...] += tally(lab)
+        blocks = [unfold(arrived.at[q, p], cap) for p in own]
         hi, lo = split(jnp.concatenate(blocks, axis=0))
         both = jnp.concatenate([hi, lo], axis=0)
         for t in range(tiles):
@@ -370,26 +410,17 @@
             forward(q, p).start()
 
     def tags_done():
-        for p in range(1, owners):
+        for p in range(last_pair, owners):
             send_tag(p).wait_recv()
         for q in range(1, reps):
             pass_tags(q).start()
 
     def counts_done():
-        for q in range(1, reps):
-            pass_tags(q).wait_recv()
-        total = jnp.sum(tags_in[...].reshape(reps * owners, width), axis=0, keepdims=True)
-        half_ref[...] = total[:, LANES:]
-        halves_ref[core] = total[:, LANES:]
-        to_half.start()
-        lab = jnp.concatenate(
-            [labels_of(q, g) for q in range(reps) for g in range(s.pairs)], axis=1
-        )
-        n = lab.shape[1]
-        up = max(SUB, s.home_rows)
-        high = onehot(iota((up, n), 0) == (lab >> 7))
-        low = onehot(iota((LANES, n), 0) == (lab & (LANES - 1)))
-        count = mm(high, low, ((1,), (1,)))
+        count = tally_ref[...]
+        for q in range(reps):
+            if q:
+                pass_tags(q).wait_recv()
+            count = count + tally(place_of([tags_in[q, i] for i in range(s.pair)]))
         count_ref[...] = count[: s.home_rows]
         scale = 1.0 / jnp.sqrt(1.0 + count)
         for k in range(s.home_rows):
@@ -402,64 +433,51 @@
                 forward(q, p).wait_recv()
             add(q, g, last=last and q == reps - 1)
 
-    chunks = owners // nb
-    half = owners // 2
-    held = range(owners - owners // 8, owners)
-    make_tags()
-    loads[4].wait()
-    feat_hi, feat_lo = split(feat_ref[...])
-    for c in range(chunks):
+    unit = s.pair // 2
+    feats = []
+
+    def pack(c):
+        if c == 0:
+            loads[4].wait()
+            feats.extend(split(feat_ref[...]))
         place = onehot(iota((width, rows), 0) + c * width == slot)
-        packed = mm(place, feat_hi) + mm(place, feat_lo)
+        packed = mm(place, feats[0]) + mm(place, feats[1])
         for i in range(nb):
             p = c * nb + i
-            dst = arrived.at[0, 0] if p == 0 else bucket.at[p - 1]
-            dst[...] = packed[i * cap : (i + 1) * cap]
-        if c == 0:
-            pl.semaphore_wait(barrier, owners + reps - 2)
-        for p in range(c * nb, (c + 1) * nb):
-            if p == 0:
-                pass_on(0)
-            elif p not in held:
-                send_block(p).start()
-        if c == 0:
-            for p in range(1, owners):
-                send_tag(p).start()
-        if c == 1:
-            hot_start()
-
-    quarter = half // 2
-    pairs = s.pairs
-    for p in range(1, quarter):
-        pass_on(p)
-    hot_1()
-    for p in range(quarter, half):
-        pass_on(p)
-    tags_done()
-    for g in range(pairs // 4):
-        add(0, g, first=g == 0)
-    hot_2()
-    for g in range(pairs // 4, pairs // 2):
-        add(0, g)
-    hot_3()
-    for p in held:
-        send_block(p).start()
-    counts_done()
-    peers(0)
-    for g in range(pairs // 2, pairs):
-        for p in range(g * s.pair, (g + 1) * s.pair):
+            for k in range(s.parts):
+                part = packed[i * cap : (i + 1) * cap, k * LANES : (k + 1) * LANES]
+                block_of(p)[k * cap : (k + 1) * cap] = part
+
+    def send(u):
+        for p in range(max(1, u * unit), (u + 1) * unit):
+            send_block(p).start()
+
+    def follow(u):
+        for p in range(u * unit, (u + 1) * unit):
             pass_on(p)
-        if g == pairs // 2:
-            hot_4()
-        if g == pairs - 2:
-            hot_5()
-        if g > pairs // 2:
-            add(0, g - 1)
-            peers(g - pairs // 2)
-    add(0, pairs - 1)
-    hot_6()
-    for g in range(pairs // 2, pairs):
-        peers(g, last=g == pairs - 1)
+
+    def send_tags():
+        for p in range(last_pair, owners):
+            send_tag(p).start()
+
+    def enter():
+        pl.semaphore_wait(barrier, owners + reps - 2)
+
+    steps = {
+        "M": lambda n: make_tags(),
+        "K": pack,
+        "B": lambda n: enter(),
+        "s": send,
+        "f": follow,
+        "t": lambda n: send_tags(),
+        "T": lambda n: tags_done(),
+        "C": lambda n: counts_done(),
+        "a": lambda n: add(0, n, first=n == 0),
+        "p": lambda n: peers(n, last=n == s.pairs - 1),
+        "H": lambda n: (hot_start, hot_1, hot_2, hot_3, hot_4, hot_5, hot_6)[n](),
+    }
+    for step in PLAN:
+        steps[step[0]](int(step[1:]))
 
     to_core.wait_send()
     for d in range(1, s.near):
@@ -471,13 +489,21 @@
     for f in range(1, s.far):
         to_far(f).wait_send()
     to_mate.wait_send()
-    to_half.wait_send()
-    sent = tags.at[pl.ds(1, owners - 1)]
-    pltpu.make_async_copy(sent, sent, tsend).wait()
+    pltpu.make_async_copy(tags, tags, tsend).wait()
     pltpu.make_async_copy(bucket, bucket, send1).wait()
     if reps > 1:
         sent = arrived.at[pl.ds(1, reps - 1)]
         pltpu.make_async_copy(sent, sent, send2).wait()
+
+
+def write_out(*refs):
+    n = len(refs) // 2
+    sems = refs[-1]
+    copies = [pltpu.make_async_copy(refs[i], refs[n + i], sems.at[i]) for i in range(n)]
+    for copy in copies:
+        copy.start()
+    for copy in copies:
+        copy.wait()
 
 
 def local(features, group_ids, survive, home_row, hot_ids):
@@ -497,7 +523,7 @@
         features,
     )
     operands = [pltpu.with_memory_space_constraint(x, pltpu.HBM) for x in operands]
-    cold_sum, count, hot_sum, hot_count = pl.pallas_call(
+    results = pl.pallas_call(
         functools.partial(kernel, s),
         out_shape=(
             pltpu.VMEM((s.home_dev, width), F32),
@@ -513,45 +539,51 @@
             VM((1, hots), jnp.int32),
             VM((groups // LANES, LANES), jnp.int32),
             VM((rows, width), F32),
-            VM((owners - 1, s.cap, width), F32),
-            VM((reps, owners, s.cap, width), F32),
-            VM((owners, 1, width), F32),
-            VM((reps, owners, 1, width), F32),
+            VM((owners - 1, s.block, LANES), F32),
+            VM((reps, owners, s.block, LANES), F32),
+            VM((s.pair, 1, LANES), F32),
+            VM((reps, s.pair, 1, LANES), F32),
+            VM((s.count_rows, LANES), F32),
             VM((s.home_dev, LANES), F32),
-            VM((2, s.near, reps, s.piece, width), F32),
-            VM((s.near, reps, s.piece, width), F32),
-            VM((s.near, reps, s.piece, width), F32),
-            VM((s.near, reps, s.piece, width), F32),
-            VM((reps, s.piece, width), F32),
-            VM((reps, s.piece, width), F32),
-            VM((s.piece, width), F32),
-            VM((s.far, s.piece, width), F32),
-            VM((s.piece, width), F32),
-            VM((2, s.near, s.piece, width), F32),
-            VM((1, LANES), F32),
-            VM((2, 1, LANES), F32),
+            VM((2, s.near, reps, s.hot_block, LANES), F32),
+            VM((s.near, reps, s.hot_block, LANES), F32),
+            VM((s.near, reps, s.hot_block, LANES), F32),
+            VM((s.near, reps, s.hot_block, LANES), F32),
+            VM((reps, s.hot_block, LANES), F32),
+            VM((reps, s.hot_block, LANES), F32),
+            VM((s.hot_block, LANES), F32),
+            VM((s.far, s.hot_block, LANES), F32),
+            VM((s.hot_block, LANES), F32),
+            VM((2, s.near, s.hot_block, LANES), F32),
             DMA((5,)),
             DMA(()),
             DMA((owners,)),
             DMA(()),
             DMA((reps, owners)),
             DMA(()),
-            DMA((owners,)),
+            DMA((s.pair,)),
             DMA(()),
             DMA((reps,)),
-            DMA((7,)),
+            DMA((6,)),
             DMA(()),
             DMA((s.near,)),
             DMA((reps,)),
             DMA((s.far,)),
             DMA((s.near,)),
             DMA(()),
-            DMA(()),
         ],
         compiler_params=pltpu.CompilerParams(
             collective_id=0, has_side_effects=True, vmem_limit_bytes=48 << 20
         ),
     )(*operands)
+    results = [pltpu.with_memory_space_constraint(x, pltpu.VMEM) for x in results]
+    cold_sum, count, hot_sum, hot_count = pl.pallas_call(
+        write_out,
+        out_shape=[jax.ShapeDtypeStruct(x.shape, x.dtype) for x in results],
+        in_specs=[vmem] * 4,
+        out_specs=[hbm] * 4,
+        scratch_shapes=[DMA((4,))],
+    )(*results)
     return cold_sum, count.reshape(s.home_dev), hot_sum, hot_count.reshape(hots // reps)
 
 

time: 45.8 us -> 38.8 us (0.85)
  Pallas kernels: 41.9 us -> 38 us
  local copies, waits for them, and re-layouts: 3.09 us -> 0 us
    pallas_call x1, Pallas kernels: 41.9 us -> 36.6 us  [local(): pl.pallas_call(functools.partial(kernel, s), out_shape=(pltpu.VMEM((s.hom...]
    unnamed x4 -> x0, local copies, waits for them, and re-layouts: 3.09 us -> none
    pallas_call x0 -> x1, Pallas kernels: none -> 1.39 us  [local(): pl.pallas_call(write_out, out_shape=[jax.ShapeDtypeStruct(x.shape, x.dtyp...]
where the time goes in v2:
time: 38.8 us; the launch traced here: 38.7 us
  Pallas kernels  38 us (98%)
  between operations  0.64 us (2%)
    pallas_call x1, Pallas kernels, local(): pl.pallas_call(functools.partial(kernel, s), out_shape=(pltpu.VMEM((s.hom...  36.6 us
    pallas_call x1, Pallas kernels, local(): pl.pallas_call(write_out, out_shape=[jax.ShapeDtypeStruct(x.shape, x.dtyp...  1.39 us

profile of v2, /device:TPU:0, one launch (start us, length us, event | category | flops | bytes accessed | tf_op | source)
XLA Modules:
  0.0 38.7 jit_solution(3937942657643709080)
XLA Ops:
  0.6 36.6 %shard_map.84 = (f32[2048,256]{1,0:T(8,128)S(1)}, f32[16,128]{1,0:T(8,128)S(1)}, f32[128,256]{1,0:T(8,128)S(1)}, f32[1,128]{1,0:T(1,128)S(1)}) custom-call(s32[1,512]{1,0:T(1,128)} %bitcast.7, s32[1,512]{1,0:T(1,128)} %bitcast.8, s32[1,256]{1,0:T(1,128)} %bitcast.9, s32[512,128]{1,0:T(8,128)} %bitcast.6, f32[512,256]{1,0:T(8,128)} %feat_hbm.1), custom_call_target="tpu_custom_call" | custom-call | tf_op jit(solution)/shard_map/pallas_call | solution.py:526
  37.3 1.4 %shard_map.85 = (f32[2048,256]{1,0:T(8,128)}, f32[16,128]{1,0:T(8,128)}, f32[128,256]{1,0:T(8,128)}, f32[1,128]{1,0:T(1,128)}) custom-call(f32[2048,256]{1,0:T(8,128)S(1)} %get-tuple-element.12.refs_0_, f32[16,128]{1,0:T(8,128)S(1)} %get-tuple-element.13.refs_1_, f32[128,256]{1,0:T(8,128)S(1)} %get-tuple-element.14.refs_2_, ...), custom_call_target="tpu_custom_call" | custom-call | tf_op jit(solution)/shard_map/pallas_call | solution.py:580

commit v3 on v2

--- a/solution.py
+++ b/solution.py
@@ -36,12 +36,18 @@
 
 
 PLAN = (
-    "M0", "K0", "B0", "s1", "s2", "s3", "f0", "t0", "K1", "s4", "H0", "s5",
-    "s6", "s7", "K2", "s8", "s9", "K3", "s10", "s11", "f1", "f2", "f3", "H1",
-    "s12", "s13", "f4", "f5", "f6", "f7", "T0", "a0", "a1", "a2", "H2", "f11",
-    "a3", "f9", "H3", "s14", "s15", "f10", "f8", "a4", "f12", "f13", "p2", "H4",
-    "p0", "f14", "f15", "a7", "a6", "p1", "p3", "a5", "H5", "p4", "p5", "p6",
+    "M0", "K0", "B0", "s1", "s3", "s2", "f0", "t0", "K1", "s4", "H0", "s5",
+    "s6", "s7", "K2", "s8", "s9", "s10", "K3", "f1", "H1", "s11", "s13", "f2",
+    "f3", "f4", "f5", "f6", "s12", "f7", "T0", "a0", "a1", "H2", "f8", "f9",
+    "H3", "s14", "s15", "f10", "f11", "a2", "a3", "p0", "f12", "a4", "f13", "H4",
+    "p1", "f14", "f15", "a5", "a6", "a7", "p2", "p4", "p3", "H5", "p5", "p6",
     "C0", "H6", "p7",
+)
+
+ORDERS = (
+    (0, 1, 3, 2, 4, 5, 9, 6, 7, 8, 10, 11, 12, 13, 14, 15),
+    (0, 1, 2, 8, 3, 9, 10, 11, 4, 5, 6, 7, 12, 13, 15, 14),
+    (0, 1, 2, 8, 3, 10, 4, 9, 5, 6, 7, 12, 13, 11, 14, 15),
 )
 
 
@@ -117,6 +123,7 @@
     h_last,
 ):
     owners, reps, cap, nb = s.owners, s.reps, s.cap, s.nb
+    unit = s.pair // 2
     rows, width, hots = s.rows, s.width, s.hots
     me = lax.axis_index("owner")
     rep = lax.axis_index("rep")
@@ -239,12 +246,22 @@
     def unfold(ref, n):
         return jnp.concatenate([ref[k * n : (k + 1) * n] for k in range(s.parts)], axis=1)
 
+    spans = (pl.ds(0, s.block),)
+
     def send_block(p):
-        return remote(bucket.at[p - 1], arrived.at[0, p], send1, recv1.at[p], (partner(p), rep))
-
-    def forward(q, p):
+        for i, span in enumerate(spans):
+            remote(
+                bucket.at[p - 1, span],
+                arrived.at[0, p, span],
+                send1,
+                recv1.at[p, i],
+                (partner(p), rep),
+            ).start()
+
+    def forward(q, p, i):
+        piece = arrived.at[0, p, spans[i]]
         return remote(
-            arrived.at[0, p], arrived.at[q, p], send2, recv2.at[q, p], (me, other_rep(q))
+            piece, arrived.at[q, p, spans[i]], send2, recv2.at[q, p, i], (me, other_rep(q))
         )
 
     def send_tag(p):
@@ -403,11 +420,23 @@
                 total = total * jnp.concatenate([scale] * (width // LANES), axis=1)
             sum_ref[at, :] = total
 
-    def pass_on(p):
-        if p:
-            send_block(p).wait_recv()
-        for q in range(1, reps):
-            forward(q, p).start()
+    far_half = me // (owners // 2)
+    far_part = lax.rem(me // (owners // 4), 2)
+    outer = 1 - lax.rem(far_half + far_part, 2)
+
+    def pass_on(n):
+        u, v = n // unit, n % unit
+        inner, even, odd = (order[u] * unit + v for order in ORDERS)
+        if inner == even == odd:
+            p = inner
+        else:
+            p = inner + outer * ((even - inner) + core * (odd - even))
+        for i in range(len(spans)):
+            if n:
+                piece = arrived.at[0, p, spans[i]]
+                pltpu.make_async_copy(piece, piece, recv1.at[p, i]).wait()
+            for q in range(1, reps):
+                forward(q, p, i).start()
 
     def tags_done():
         for p in range(last_pair, owners):
@@ -430,10 +459,10 @@
     def peers(g, last=False):
         for q in range(1, reps):
             for p in range(g * s.pair, (g + 1) * s.pair):
-                forward(q, p).wait_recv()
+                for i in range(len(spans)):
+                    forward(q, p, i).wait_recv()
             add(q, g, last=last and q == reps - 1)
 
-    unit = s.pair // 2
     feats = []
 
     def pack(c):
@@ -450,7 +479,7 @@
 
     def send(u):
         for p in range(max(1, u * unit), (u + 1) * unit):
-            send_block(p).start()
+            send_block(p)
 
     def follow(u):
         for p in range(u * unit, (u + 1) * unit):
@@ -557,9 +586,9 @@
             VM((2, s.near, s.hot_block, LANES), F32),
             DMA((5,)),
             DMA(()),
-            DMA((owners,)),
+            DMA((owners, 1)),
             DMA(()),
-            DMA((reps, owners)),
+            DMA((reps, owners, 1)),
             DMA(()),
             DMA((s.pair,)),
             DMA(()),

time: 38.8 us -> 37.9 us (0.977)
  Pallas kernels: 38 us -> 37.1 us
    pallas_call x1, Pallas kernels: 36.6 us -> 35.8 us  [local(): pl.pallas_call(functools.partial(kernel, s), out_shape=(pltpu.VMEM((s.hom...]
where the time goes in v3:
time: 37.9 us; the launch traced here: 37.8 us
  Pallas kernels  37.1 us (98%)
  between operations  0.64 us (2%)
    pallas_call x1, Pallas kernels, local(): pl.pallas_call(functools.partial(kernel, s), out_shape=(pltpu.VMEM((s.hom...  35.8 us
    pallas_call x1, Pallas kernels, local(): pl.pallas_call(write_out, out_shape=[jax.ShapeDtypeStruct(x.shape, x.dtyp...  1.39 us

profile of v3, /device:TPU:0, one launch (start us, length us, event | category | flops | bytes accessed | tf_op | source)
XLA Modules:
  0.0 37.8 jit_solution(13343995197532415442)
XLA Ops:
  0.6 35.8 %shard_map.84 = (f32[2048,256]{1,0:T(8,128)S(1)}, f32[16,128]{1,0:T(8,128)S(1)}, f32[128,256]{1,0:T(8,128)S(1)}, f32[1,128]{1,0:T(1,128)S(1)}) custom-call(s32[1,512]{1,0:T(1,128)} %bitcast.7, s32[1,512]{1,0:T(1,128)} %bitcast.8, s32[1,256]{1,0:T(1,128)} %bitcast.9, s32[512,128]{1,0:T(8,128)} %bitcast.6, f32[512,256]{1,0:T(8,128)} %feat_hbm.1), custom_call_target="tpu_custom_call" | custom-call | tf_op jit(solution)/shard_map/pallas_call | solution.py:555
  36.4 1.4 %shard_map.85 = (f32[2048,256]{1,0:T(8,128)}, f32[16,128]{1,0:T(8,128)}, f32[128,256]{1,0:T(8,128)}, f32[1,128]{1,0:T(1,128)}) custom-call(f32[2048,256]{1,0:T(8,128)S(1)} %get-tuple-element.12.refs_0_, f32[16,128]{1,0:T(8,128)S(1)} %get-tuple-element.13.refs_1_, f32[128,256]{1,0:T(8,128)S(1)} %get-tuple-element.14.refs_2_, ...), custom_call_target="tpu_custom_call" | custom-call | tf_op jit(solution)/shard_map/pallas_call | solution.py:609

commit v4 on v3

--- a/solution.py
+++ b/solution.py
@@ -40,7 +40,7 @@
     "s6", "s7", "K2", "s8", "s9", "s10", "K3", "f1", "H1", "s11", "s13", "f2",
     "f3", "f4", "f5", "f6", "s12", "f7", "T0", "a0", "a1", "H2", "f8", "f9",
     "H3", "s14", "s15", "f10", "f11", "a2", "a3", "p0", "f12", "a4", "f13", "H4",
-    "p1", "f14", "f15", "a5", "a6", "a7", "p2", "p4", "p3", "H5", "p5", "p6",
+    "p1", "f14", "f15", "a5", "a6", "p2", "p4", "p3", "p5", "H5", "p6", "a7",
     "C0", "H6", "p7",
 )
 

time: 37.9 us -> 37.9 us (level)
  no operation moved by 1% of the time
where the time goes in v4:
time: 37.9 us; the launch traced here: 37.8 us
  Pallas kernels  37.1 us (98%)
  between operations  0.64 us (2%)
    pallas_call x1, Pallas kernels, local(): pl.pallas_call(functools.partial(kernel, s), out_shape=(pltpu.VMEM((s.hom...  35.8 us
    pallas_call x1, Pallas kernels, local(): pl.pallas_call(write_out, out_shape=[jax.ShapeDtypeStruct(x.shape, x.dtyp...  1.39 us

profile of v4, /device:TPU:0, one launch (start us, length us, event | category | flops | bytes accessed | tf_op | source)
XLA Modules:
  0.0 37.8 jit_solution(13484928350484620691)
XLA Ops:
  0.6 35.8 %shard_map.84 = (f32[2048,256]{1,0:T(8,128)S(1)}, f32[16,128]{1,0:T(8,128)S(1)}, f32[128,256]{1,0:T(8,128)S(1)}, f32[1,128]{1,0:T(1,128)S(1)}) custom-call(s32[1,512]{1,0:T(1,128)} %bitcast.7, s32[1,512]{1,0:T(1,128)} %bitcast.8, s32[1,256]{1,0:T(1,128)} %bitcast.9, s32[512,128]{1,0:T(8,128)} %bitcast.6, f32[512,256]{1,0:T(8,128)} %feat_hbm.1), custom_call_target="tpu_custom_call" | custom-call | tf_op jit(solution)/shard_map/pallas_call | solution.py:555
  36.4 1.4 %shard_map.85 = (f32[2048,256]{1,0:T(8,128)}, f32[16,128]{1,0:T(8,128)}, f32[128,256]{1,0:T(8,128)}, f32[1,128]{1,0:T(1,128)}) custom-call(f32[2048,256]{1,0:T(8,128)S(1)} %get-tuple-element.12.refs_0_, f32[16,128]{1,0:T(8,128)S(1)} %get-tuple-element.13.refs_1_, f32[128,256]{1,0:T(8,128)S(1)} %get-tuple-element.14.refs_2_, ...), custom_call_target="tpu_custom_call" | custom-call | tf_op jit(solution)/shard_map/pallas_call | solution.py:609
